TPU v7x, 32 devices: a whole 2x2x4 slice. The times are simulated.
32 devices in a mesh: section: 8 (over y, x, core), tp: 4 (over z).
Axes of the slice: x: 2, y: 2, z: 4, core: 2. Of those that a mesh axis runs over, the one named last changes fastest.
Arguments:
- stash: bfloat16 [8, 2, 256, 4096], P('section', None, 'tp'), may hold values from -660 to 660
- slot: int32 [8], P('section'), may hold values from 0 to 1
- doc_ids: int32 [8, 2, 256], P('section', None, 'tp'), may hold values from 0 to 3, never falling along the last dimension, each value on 1 to 128 neighbouring positions
- norm_gain: bfloat16 [4096], replicated, may hold values from 0.099609375 to 1.8984375
- w_query: bfloat16 [4096, 4096], P(None, 'tp'), may hold values from -21 to 21
- w_key: bfloat16 [4096, 1024], P(None, 'tp'), may hold values from -21 to 21
- value_weight: bfloat16 [4096, 1024], P(None, 'tp'), may hold values from -0.09375 to 0.09375
Outputs:
- received: bfloat16 [8, 256, 4096], P('section', None, 'tp')
Inputs may be any that keep to these rules, and one draw needn't show every extreme that they name: `doc_ids`: document numbers never fall along a micro-batch.
All inputs are finite; a program needn't handle non-finite values.
Results may differ from a plain program's by a relative error of at most 0.025.
The roundings to bfloat16 on the way count: a program that leaves them out, or rounds other values in their place, can miss the bound.
Values may be sent and summed in bfloat16 or wider, within the bound.
A program may use at most 64 MiB of HBM per device.

v0:
```python
import math
import jax
import jax.numpy as jnp
from jax import lax
from jax.sharding import PartitionSpec as P

HEAD_SIZE = 128
ROPE_BASE = 500000.0
NORM_EPSILON = 1e-05


def from_behind(block, axis, distance):
    devices = range(lax.axis_size(axis))
    route = [(i - distance, i) for i in devices if i - distance in devices]
    return lax.ppermute(block, axis, route)


def rotate(values, positions):
    head_width = values.shape[-1]
    half_width = head_width // 2
    freq_index = jnp.arange(half_width, dtype=jnp.float32)
    inverse = jnp.power(jnp.float32(ROPE_BASE), -2.0 * freq_index / head_width)
    angles = positions.astype(jnp.float32)[:, None] * inverse[None, :]
    cosine = jnp.concatenate([jnp.cos(angles), jnp.cos(angles)], -1)[:, None, :]
    sine_part = jnp.concatenate([jnp.sin(angles), jnp.sin(angles)], -1)[:, None, :]
    turned = jnp.concatenate([-values[..., half_width:], values[..., :half_width]], -1)
    return values * cosine + turned * sine_part


def normalize(stash_rows, norm_gain):
    widened = stash_rows.astype(jnp.float32)
    mean_square = jnp.mean(widened * widened, axis=-1, keepdims=True)
    return (widened * lax.rsqrt(mean_square + NORM_EPSILON) * norm_gain.astype(jnp.float32)).astype(
        jnp.bfloat16
    )


def project(normed, weight, positions, use_rope):
    length = normed.shape[0]
    product = jnp.dot(normed, weight, preferred_element_type=jnp.float32)
    if use_rope:
        product = rotate(product.reshape(length, -1, HEAD_SIZE), positions).reshape(length, -1)
    return product.astype(jnp.bfloat16)


def attend(queries, keys, values, doc_rows):
    length = queries.shape[0]
    kv_count = keys.shape[1] // HEAD_SIZE
    group_size = queries.shape[1] // HEAD_SIZE // kv_count
    grouped = queries.reshape(length, kv_count, group_size, HEAD_SIZE)
    key_heads = keys.reshape(length, kv_count, HEAD_SIZE)
    value_heads = values.reshape(length, kv_count, HEAD_SIZE)
    scores = jnp.einsum(
        "ihgd,jhd->hgij", grouped, key_heads, preferred_element_type=jnp.float32
    ) * (1.0 / math.sqrt(HEAD_SIZE))
    row_index = jnp.arange(length, dtype=jnp.int32)[:, None]
    col_index = jnp.arange(length, dtype=jnp.int32)[None, :]
    allowed = (col_index <= row_index) & (doc_rows[None, :] == doc_rows[:, None])
    scores = jnp.where(allowed, scores, -1e30)
    row_max = jnp.max(scores, axis=-1, keepdims=True)
    score_exponent = jnp.exp(scores - row_max)
    softmax_weights = (score_exponent / jnp.sum(score_exponent, axis=-1, keepdims=True)).astype(
        jnp.bfloat16
    )
    context = jnp.einsum(
        "hgij,jhd->ihgd", softmax_weights, value_heads, preferred_element_type=jnp.float32
    )
    return context.reshape(length, -1).astype(jnp.bfloat16)


def per_device(stash, slot, doc_ids, norm_gain, w_query, w_key, value_weight):
    group_count = lax.axis_size("tp")
    local_length = stash.shape[2]
    total_length = local_length * group_count
    chosen_slot = slot[0]
    picked = lax.dynamic_index_in_dim(stash[0], chosen_slot, 0, keepdims=False)
    doc_rows = lax.dynamic_index_in_dim(doc_ids[0], chosen_slot, 0, keepdims=False)
    doc_all = jnp.zeros((total_length,), jnp.int32)
    piece_rows = lax.all_gather(picked, "tp", axis=0, tiled=True)
    piece_docs = lax.all_gather(doc_rows, "tp", axis=0, tiled=True)
    piece_count = piece_rows.shape[0]
    positions = jnp.arange(piece_count, dtype=jnp.int32)
    normed = normalize(piece_rows, norm_gain)
    queries = project(normed, w_query, positions, True)
    keys = project(normed, w_key, positions, True)
    values = project(normed, value_weight, positions, False)
    doc_all = lax.dynamic_update_slice_in_dim(doc_all, piece_docs, jnp.int32(0), 0)
    queries, keys, values, doc_all = (queries, keys, values, doc_all)
    context = attend(queries, keys, values, doc_all)
    return from_behind(context[None], "section", 1)


def solution(mesh):
    placed = (
        P("section", None, "tp", None),
        P("section"),
        P("section", None, "tp"),
        P(),
        P(None, "tp"),
        P(None, "tp"),
        P(None, "tp"),
    )
    return jax.shard_map(
        per_device, mesh=mesh, in_specs=placed, out_specs=P("section", None, "tp"), check_vma=False
    )
```

profile of v0, /device:TPU:4, one launch (start us, length us, event | category | flops | bytes accessed | tf_op | source)
XLA Modules:
  0.0 92.8 jit_solution(12643340829580763346)
XLA Ops:
  7.3 1.9 %constant_dynamic-slice_fusion = bf16[1,1,64,4096]{3,2,1,0:T(8,128)(2,1)} fusion(bf16[1,2,64,4096]{3,2,1,0:T(8,128)(2,1)} %param.7, s32[]{:T(128)S(6)} %select_n.10), kind=kLoop, calls=%fused_computation.37 | loop fusion | bytes 1048580 | tf_op jit(solution)/shard_map/jit(dynamic_index_in_dim)/dynamic_slice | solution.py:76
  9.3 0.7 convert_element_type.52
  10.0 0.3 multiply_cosine_fusion
  10.4 0.1 copy.8
  10.5 0.6 dynamic-slice.2
  11.7 0.1 bitcast_dynamic-update-slice_fusion
  11.8 8.4 %all-reduce = s32[256]{0:T(256)S(1)} all-reduce(s32[256]{0:T(256)S(1)} %bitcast_dynamic-update-slice_fusion), channel_id=3, replica_groups=mesh['section'=8,'tp'=4] {'tp'}, use_global_device_ids=true, to_apply=%add | all-reduce | flops 256 | bytes 2048 | tf_op jit(solution)/shard_map/all_gather | solution.py:80
  20.2 0.1 fusion.12
  20.3 35.9 %all-gather.4.cloned.1.call-done = bf16[1,1,256,4096]{3,2,1,0:T(8,128)(2,1)} async-done(((bf16[1,1,64,4096]{3,2,1,0:T(8,128)(2,1)}), bf16[1,1,256,4096]{3,2,1,0:T(8,128)(2,1)}) %all-gather.4.cloned.1.call-update) | async-done | bytes 2097168 | tf_op jit(solution)/shard_map/all_gather | solution.py:79
  56.3 2.2 %fusion.1 = f32[256]{0:T(256)S(1)} fusion(bf16[1,1,256,4096]{3,2,1,0:T(8,128)(2,1)} %all-gather.4.cloned.1.call-done), kind=kLoop, calls=%fused_computation.3 | loop fusion | flops 3145472 | bytes 2098176 | tf_op jit(solution)/shard_map/reduce_sum | solution.py:32
  58.5 1.1 %fusion.23 = f32[256,256]{0,1:T(8,128)S(1)} fusion(bf16[4096,256]{1,0:T(8,128)(2,1)S(1)} %copy-done, bf16[1,1,256,4096]{3,2,1,0:T(8,128)(2,1)S(1)} %copy-done.1, f32[4096]{0:T(1024)S(1)} %convert_element_type.52, f32[256]{0:T(256)S(1)} %add_rsqrt_fusion), kind=kOutput, calls=%fused_computation.41 | convolution fusion | flops 541065216 | bytes 4473856 | tf_op jit(solution)/shard_map/dot_general | solution.py:40
  59.8 5.7 %fusion.21 = f32[256,1024]{1,0:T(8,128)S(1)} fusion(bf16[4096,1024]{1,0:T(8,128)(2,1)} %param.11, bf16[1,1,256,4096]{3,2,1,0:T(8,128)(2,1)S(1)} %copy-done.1, f32[4096]{0:T(1024)S(1)} %convert_element_type.52, f32[256]{0:T(256)S(1)} %add_rsqrt_fusion), kind=kOutput, calls=%fused_computation.40 | convolution fusion | flops 2151677952 | bytes 11551744 | tf_op jit(solution)/shard_map/dot_general | solution.py:40
  65.5 0.2 copy.20
  65.7 0.3 slice_negate_fusion
  66.1 0.4 maximum_multiply_fusion
  66.5 0.6 fusion.5
  67.1 0.4 reshape.69
  67.5 2.2 %fusion.26 = (f32[2,4,256]{2,1,0:T(4,128)S(1)}, f32[2,4,256,256]{2,3,1,0:T(8,128)}) fusion(pred[256,256]{0,1:T(8,128)(4,1)S(1)} %fusion.12, bf16[256,2,128,1]{0,2,3,1:T(8,128)(2,1)S(1)} %bitcast.66, bf16[256,2,4,128]{3,2,1,0:T(4,128)(2,1)S(1)} %reshape.69), kind=kOutput, calls=%fused_computation.42 | convolution fusion | flops 136315136 | bytes 2826240 | tf_op jit(solution)/shard_map/sub | solution.py:61
  69.7 3.5 %convolution_convert_fusion.1 = bf16[256,256]{0,1:T(8,128)(2,1)S(1)} fusion(bf16[4096,256]{1,0:T(8,128)(2,1)} %param.13, bf16[1,1,256,4096]{3,2,1,0:T(8,128)(2,1)} %all-gather.4.cloned.1.call-done, f32[4096]{0:T(1024)S(1)} %convert_element_type.52, f32[256]{0:T(256)S(1)} %add_rsqrt_fusion), kind=kOutput, calls=%fused_computation.11 | convolution fusion | flops 541130752 | bytes 4342784 | tf_op jit(solution)/shard_map/dot_general | solution.py:40
  73.2 0.3 convolution_convert_fusion
  73.6 0.2 copy.13
  73.8 1.9 %collective-permute-start = (bf16[1,256,1024]{2,1,0:T(8,128)(2,1)S(1)}, bf16[1,256,1024]{2,1,0:T(8,128)(2,1)S(1)}, u32[]{:S(2)}, u32[]{:S(2)}) collective-permute-start(bf16[1,256,1024]{2,1,0:T(8,128)(2,1)S(1)} %copy.13), channel_id=1, source_target_pairs={{0,4},{4,8},{8,12},{12,16},{16,20},{20,24},{24,28},{1,5},{5,9},{9,... | collective-permute-start | bytes 1572872 | tf_op jit(solution)/shard_map/ppermute | solution.py:15
  75.7 9.5 %collective-permute-done = bf16[1,256,1024]{2,1,0:T(8,128)(2,1)S(1)} collective-permute-done((bf16[1,256,1024]{2,1,0:T(8,128)(2,1)S(1)}, bf16[1,256,1024]{2,1,0:T(8,128)(2,1)S(1)}, u32[]{:S(2)}, u32[]{:S(2)}) %collective-permute-start) | collective-permute-done | bytes 524320 | tf_op jit(solution)/shard_map/ppermute | solution.py:15
  85.2 0.8 copy.37
  (22 shorter events, 0.3 us)
Async XLA Ops:
  6.5 52.0 %copy-start = (bf16[4096,256]{1,0:T(8,128)(2,1)S(1)}, bf16[4096,256]{1,0:T(8,128)(2,1)}, u32[]{:S(2)}) copy-start(bf16[4096,256]{1,0:T(8,128)(2,1)} %param.12) | copy-start | bytes 6291460
  6.5 4.0 %copy-start.3 = (u32[32]{0:T(128)S(1)}, u32[32]{0:T(128)}, u32[]{:S(2)}) copy-start(u32[32]{0:T(128)} %constant.37) | copy-start | bytes 388
  6.5 5.1 %copy-start.2 = (s32[1,2,64]{2,1,0:T(2,128)S(1)}, s32[1,2,64]{2,1,0:T(2,128)}, u32[]{:S(2)}) copy-start(s32[1,2,64]{2,1,0:T(2,128)} %param.9) | copy-start | bytes 1540
  6.5 49.7 %all-gather.4.cloned.1.call-start = ((), (), s32[]{:S(2)}) async-start(), calls=%async_computation | async-start | bytes 2621440 | tf_op jit(solution)/shard_map/all_gather | solution.py:79
  56.3 2.3 %copy-start.1 = (bf16[1,1,256,4096]{3,2,1,0:T(8,128)(2,1)S(1)}, bf16[1,1,256,4096]{3,2,1,0:T(8,128)(2,1)}, u32[]{:S(2)}) copy-start(bf16[1,1,256,4096]{3,2,1,0:T(8,128)(2,1)} %all-gather.4.cloned.1.call-done) | copy-start | bytes 6291460
  69.7 3.5 %copy-start.4 = (f32[2,4,256,256]{2,3,1,0:T(8,128)S(1)}, f32[2,4,256,256]{2,3,1,0:T(8,128)}, u32[]{:S(2)}) copy-start(f32[2,4,256,256]{2,3,1,0:T(8,128)} %get-tuple-element.12) | copy-start | bytes 6291460
  73.8 11.4 %collective-permute-start = (bf16[1,256,1024]{2,1,0:T(8,128)(2,1)S(1)}, bf16[1,256,1024]{2,1,0:T(8,128)(2,1)S(1)}, u32[]{:S(2)}, u32[]{:S(2)}) collective-permute-start(bf16[1,256,1024]{2,1,0:T(8,128)(2,1)S(1)} %copy.13), channel_id=1, source_target_pairs={{0,4},{4,8},{8,12},{12,16},{16,20},{20,24},{24,28},{1,5},{5,9},{9,... | collective-permute-start | bytes 1572872 | tf_op jit(solution)/shard_map/ppermute | solution.py:15
Sparse Core Ops, SparseCore 0:
  9.4 46.8 all-gather.3
where the time goes:
time: 93.1 us; the launch traced here: 92.8 us
  waiting for transfers between devices  45.4 us (49%)
  between operations  15 us (16%)
  matrix products  12.9 us (14%)
  blocking collectives  8.44 us (9%)
  other arithmetic  4.79 us (5%)
  local copies, waits for them, and re-layouts  4.37 us (5%)
  starting transfers between devices  1.92 us (2%)
    all_gather x1, waiting for transfers between devices, per_device(): piece_rows = lax.all_gather(picked, 'tp', axis=0, tiled=True)  35.9 us
    dot_general x3, matrix products, project(): product = jnp.dot(normed, weight, preferred_element_type=jnp.float32)  10.4 us
    ppermute x1, waiting for transfers between devices, from_behind(): return lax.ppermute(block, axis, route)  9.47 us
    all_gather x1, blocking collectives, per_device(): piece_docs = lax.all_gather(doc_rows, 'tp', axis=0, tiled=True)  8.44 us
    reduce_sum x1, other arithmetic, normalize(): mean_square = jnp.mean(widened * widened, axis=-1, keepdims=True)  2.23 us
    sub x1, matrix products, attend(): score_exponent = jnp.exp(scores - row_max)  2.19 us
    ppermute x1, starting transfers between devices, from_behind(): return lax.ppermute(block, axis, route)  1.92 us
    dynamic_slice x1, local copies, waits for them, and re-layouts, per_device(): picked = lax.dynamic_index_in_dim(stash[0], chosen_slot, 0, keepdims=False)  1.87 us
  transfers between devices with their start and end apart: 2, of which 2 were waited for; matrix products, arithmetic and copies ran while one was open for 2% of the time, Pallas kernels for 0%

commit v1 on v0

--- a/solution.py
+++ b/solution.py
@@ -76,7 +76,14 @@
     picked = lax.dynamic_index_in_dim(stash[0], chosen_slot, 0, keepdims=False)
     doc_rows = lax.dynamic_index_in_dim(doc_ids[0], chosen_slot, 0, keepdims=False)
     doc_all = jnp.zeros((total_length,), jnp.int32)
-    piece_rows = lax.all_gather(picked, "tp", axis=0, tiled=True)
+    peers = lax.axis_size("tp")
+    route_2 = [(i_2, (i_2 + 1) % peers) for i_2 in range(peers)]
+    shards = [picked]
+    for far in range(1, peers):
+        shards = [lax.ppermute(shards[0], "tp", route_2), *shards]
+    full = jnp.concatenate(shards, axis=0)
+    shift = (lax.axis_index("tp") + 1) * shards[-1].shape[0]
+    piece_rows = jnp.roll(full, shift, axis=0)
     piece_docs = lax.all_gather(doc_rows, "tp", axis=0, tiled=True)
     piece_count = piece_rows.shape[0]
     positions = jnp.arange(piece_count, dtype=jnp.int32)

time: 93.1 us -> 85 us (0.913)
  between operations: 15 us -> 1.75 us
  local copies, waits for them, and re-layouts: 4.37 us -> 14.5 us
  waiting for transfers between devices: 45.4 us -> 36.8 us
  blocking collectives: 8.44 us -> 11.3 us
  matrix products: 12.9 us -> 10.6 us
  starting transfers between devices: 1.92 us -> 3.55 us
  other arithmetic: 4.79 us -> 5.98 us
    all_gather x1 -> x0, waiting for transfers between devices: 35.9 us -> none  [per_device(): piece_rows = lax.all_gather(picked, 'tp', axis=0, tiled=True)]
    ppermute x0 -> x3, waiting for transfers between devices: none -> 27.4 us  [per_device(): shards = [lax.ppermute(shards[0], 'tp', route_2), *shards]]
    unnamed x15 -> x32, local copies, waits for them, and re-layouts: 1.67 us -> 11.8 us
    dot_general x3, matrix products: 10.4 us -> 6.45 us  [project(): product = jnp.dot(normed, weight, preferred_element_type=jnp.float32)]
    all_gather x1, blocking collectives: 8.44 us -> 11.3 us  [per_device(): piece_docs = lax.all_gather(doc_rows, 'tp', axis=0, tiled=True)]
    dynamic_slice x1 -> x0, local copies, waits for them, and re-layouts: 1.87 us -> none  [per_device(): picked = lax.dynamic_index_in_dim(stash[0], chosen_slot, 0, keepdims=False)]
    reduce_sum x1, other arithmetic: 2.23 us -> 0.5 us  [normalize(): mean_square = jnp.mean(widened * widened, axis=-1, keepdims=True)]
    ppermute x0 -> x3, starting transfers between devices: none -> 1.63 us  [per_device(): shards = [lax.ppermute(shards[0], 'tp', route_2), *shards]]
  transfers between devices with their start and end apart: 2 -> 4, of which waited for: 2 -> 3; matrix products, arithmetic and copies ran while one was open for 2% -> 10% of each run, Pallas kernels for 0% -> 0%
where the time goes in v1:
time: 85 us; the launch traced here: 84.5 us
  waiting for transfers between devices  36.8 us (43%)
  local copies, waits for them, and re-layouts  14.5 us (17%)
  blocking collectives  11.3 us (13%)
  matrix products  10.6 us (12%)
  other arithmetic  5.98 us (7%)
  starting transfers between devices  3.55 us (4%)
  between operations  1.75 us (2%)
    ppermute x3, waiting for transfers between devices, per_device(): shards = [lax.ppermute(shards[0], 'tp', route_2), *shards]  27.4 us
    unnamed x32, local copies, waits for them, and re-layouts  11.8 us
    all_gather x1, blocking collectives, per_device(): piece_docs = lax.all_gather(doc_rows, 'tp', axis=0, tiled=True)  11.3 us
    ppermute x1, waiting for transfers between devices, from_behind(): return lax.ppermute(block, axis, route)  9.47 us
    dot_general x3, matrix products, project(): product = jnp.dot(normed, weight, preferred_element_type=jnp.float32)  6.45 us
    sub x1, matrix products, attend(): score_exponent = jnp.exp(scores - row_max)  2.24 us
    ppermute x1, starting transfers between devices, from_behind(): return lax.ppermute(block, axis, route)  1.92 us
    dot_general x1, matrix products, attend(): jnp.einsum('hgij,jhd->ihgd', softmax_weights, value_heads, preferred_elem...  1.91 us
  transfers between devices with their start and end apart: 4, of which 3 were waited for; matrix products, arithmetic and copies ran while one was open for 10% of the time, Pallas kernels for 0%

profile of v1, /device:TPU:4, one launch (start us, length us, event | category | flops | bytes accessed | tf_op | source)
XLA Modules:
  0.0 84.5 jit_solution(6653867898233670130)
XLA Ops:
  0.8 1.1 %dynamic-slice_bitcast_fusion = bf16[64,4096]{1,0:T(8,128)(2,1)S(1)} fusion(bf16[1,2,64,4096]{3,2,1,0:T(8,128)(2,1)} %param.7, s32[]{:T(128)S(6)} %select_n.23), kind=kLoop, calls=%fused_computation.22 | loop fusion | bytes 1048580 | tf_op jit(solution)/shard_map/jit(dynamic_index_in_dim)/squeeze | solution.py:76
  2.0 1.6 %collective-permute-start = (bf16[64,4096]{1,0:T(8,128)(2,1)S(1)}, bf16[64,4096]{1,0:T(8,128)(2,1)}, u32[]{:S(2)}, u32[]{:S(2)}) collective-permute-start(bf16[64,4096]{1,0:T(8,128)(2,1)S(1)} %dynamic-slice_bitcast_fusion), channel_id=1, source_target_pairs={{0,1},{1,2},{2,3},{3,0},{4,5},{5,6},{6,7},{7,4},{8,9},{9,10},{10,1... | collective-permute-start | bytes 1572872 | tf_op jit(solution)/shard_map/ppermute | solution.py:83
  3.6 14.1 %collective-permute-done = bf16[64,4096]{1,0:T(8,128)(2,1)} collective-permute-done((bf16[64,4096]{1,0:T(8,128)(2,1)S(1)}, bf16[64,4096]{1,0:T(8,128)(2,1)}, u32[]{:S(2)}, u32[]{:S(2)}) %collective-permute-start) | collective-permute-done | bytes 524320 | tf_op jit(solution)/shard_map/ppermute | solution.py:83
  18.4 0.9 %multiply_cosine_fusion = (f32[256,64]{0,1:T(8,128)}, f32[256,64]{0,1:T(8,128)S(1)}) fusion(f32[64]{0:T(128)S(1)} %multiply_power_fusion, f32[256]{0:T(256)S(1)} %iota_convert_fusion), kind=kLoop, calls=%fused_computation.33 | loop fusion | flops 16384 | bytes 132352 | tf_op jit(solution)/shard_map/cos | solution.py:24
  19.3 13.3 %collective-permute-done.1 = bf16[64,4096]{1,0:T(8,128)(2,1)} collective-permute-done((bf16[64,4096]{1,0:T(8,128)(2,1)}, bf16[64,4096]{1,0:T(8,128)(2,1)}, u32[]{:S(2)}, u32[]{:S(2)}) %collective-permute-start.1) | collective-permute-done | bytes 524320 | tf_op jit(solution)/shard_map/ppermute | solution.py:83
  32.7 0.9 %pad_maximum_fusion = f32[256,128]{0,1:T(8,128)S(1)} fusion(f32[256,64]{0,1:T(8,128)} %get-tuple-element.9), kind=kLoop, calls=%fused_computation.30 | loop fusion | flops 32768 | bytes 196608 | tf_op jit(solution)/shard_map/concatenate | solution.py:24
  34.4 1.3 %dynamic-slice.2 = u32[1]{0:T(128)} dynamic-slice(u32[32]{0:T(128)} %constant.66, u32[]{:T(128)S(6)} %add.46), dynamic_slice_sizes={1} | dynamic-slice | bytes 12
  36.9 1.3 %fusion.18 = s32[256]{0:T(256)} fusion(s32[256]{0:T(256)} %broadcast.42, u32[]{:T(128)} %bitcast.6, s32[1,2,64]{2,1,0:T(2,128)} %param.9, s32[]{:T(128)S(6)} %select_n.23), kind=kLoop, calls=%fused_computation.46 | loop fusion | bytes 1540
  38.2 11.3 %all-reduce = s32[256]{0:T(256)} all-reduce(s32[256]{0:T(256)} %fusion.18), channel_id=2, replica_groups=mesh['section'=8,'tp'=4] {'tp'}, use_global_device_ids=true, to_apply=%add | all-reduce | flops 256 | bytes 2048 | tf_op jit(solution)/shard_map/all_gather | solution.py:87
  49.5 1.5 %fusion.12 = pred[256,256]{0,1:T(8,128)(4,1)} fusion(s32[256]{0:T(256)} %all-reduce), kind=kLoop, calls=%fused_computation.28 | loop fusion | flops 196608 | bytes 66560 | tf_op jit(solution)/shard_map/and | solution.py:58
  51.0 1.1 %constant_dynamic-update-slice_fusion.7 = bf16[512,4096]{1,0:T(8,128)(2,1)S(1)} fusion(bf16[64,4096]{1,0:T(8,128)(2,1)} %collective-permute-done.2), kind=kLoop, calls=%fused_computation.41 | loop fusion | bytes 1048576
  52.1 1.1 %constant_dynamic-update-slice_fusion.6 = bf16[512,4096]{1,0:T(8,128)(2,1)S(1)} fusion(bf16[512,4096]{1,0:T(8,128)(2,1)S(1)} %constant_dynamic-update-slice_fusion.7, bf16[64,4096]{1,0:T(8,128)(2,1)} %collective-permute-done.1), kind=kLoop, calls=%fused_computation.40 | loop fusion | bytes 1048576
  53.2 1.2 %constant_dynamic-update-slice_fusion.5 = bf16[512,4096]{1,0:T(8,128)(2,1)S(1)} fusion(bf16[512,4096]{1,0:T(8,128)(2,1)S(1)} %constant_dynamic-update-slice_fusion.6, bf16[64,4096]{1,0:T(8,128)(2,1)} %collective-permute-done), kind=kLoop, calls=%fused_computation.39 | loop fusion | bytes 1048576
  54.4 1.3 %constant_dynamic-update-slice_fusion.3 = bf16[512,4096]{1,0:T(8,128)(2,1)S(1)} fusion(bf16[512,4096]{1,0:T(8,128)(2,1)S(1)} %constant_dynamic-update-slice_fusion.4, bf16[64,4096]{1,0:T(8,128)(2,1)} %collective-permute-done.2), kind=kLoop, calls=%fused_computation.37 | loop fusion | bytes 1048576
  55.8 1.1 %constant_dynamic-update-slice_fusion.2 = bf16[512,4096]{1,0:T(8,128)(2,1)S(1)} fusion(bf16[512,4096]{1,0:T(8,128)(2,1)S(1)} %constant_dynamic-update-slice_fusion.3, bf16[64,4096]{1,0:T(8,128)(2,1)} %collective-permute-done.1), kind=kLoop, calls=%fused_computation.36 | loop fusion | bytes 1048576
  56.9 1.1 %constant_dynamic-update-slice_fusion.1 = bf16[512,4096]{1,0:T(8,128)(2,1)S(1)} fusion(bf16[512,4096]{1,0:T(8,128)(2,1)S(1)} %constant_dynamic-update-slice_fusion.2, bf16[64,4096]{1,0:T(8,128)(2,1)} %collective-permute-done), kind=kLoop, calls=%fused_computation.35 | loop fusion | bytes 1048576
  58.6 2.4 %fusion.23 = f32[256,1024]{1,0:T(8,128)S(1)} fusion(bf16[4096,1024]{1,0:T(8,128)(2,1)S(1)} %copy-done.8, f32[4096]{0:T(1024)S(1)} %convert_element_type.52, f32[256]{0:T(256)S(1)} %add_rsqrt_fusion, bf16[512,4096]{1,0:T(8,128)(2,1)S(1)} %constant_dynamic-update-slice_fusion, s32[]{:T(128)S(6)} %select_n.25), kind=kOutput, calls=%fused_computation.50 | convolution fusion | flops 2151677952 | bytes 11551748 | tf_op jit(solution)/shard_map/dot_general | solution.py:40
  63.2 2.9 %fusion.25 = f32[256,256]{0,1:T(8,128)S(1)} fusion(bf16[4096,256]{1,0:T(8,128)(2,1)S(1)} %copy-done, f32[4096]{0:T(1024)S(1)} %convert_element_type.52, f32[256]{0:T(256)S(1)} %copy-done.7, bf16[512,4096]{1,0:T(8,128)(2,1)} %copy-done.2, s32[]{:T(128)S(6)} %select_n.25), kind=kOutput, calls=%fused_computation.51 | convolution fusion | flops 541065216 | bytes 4473860 | tf_op jit(solution)/shard_map/dot_general | solution.py:40
  66.7 1.2 %convolution_convert_fusion.1 = bf16[256,256]{0,1:T(8,128)(2,1)S(1)} fusion(bf16[4096,256]{1,0:T(8,128)(2,1)S(1)} %copy-done.9, f32[4096]{0:T(1024)S(1)} %convert_element_type.52, f32[256]{0:T(256)S(1)} %copy-done.7, bf16[512,4096]{1,0:T(8,128)(2,1)S(1)} %copy-done.3, s32[]{:T(128)S(6)} %select_n.25), kind=kOutput, calls=%fused_computation.11 | convolution fusion | flops 541130752 | bytes 4342788 | tf_op jit(solution)/shard_map/dot_general | solution.py:40
  67.9 2.2 %fusion.28 = (f32[2,4,256]{2,1,0:T(4,128)S(1)}, f32[2,4,256,256]{2,3,1,0:T(8,128)}) fusion(pred[256,256]{0,1:T(8,128)(4,1)S(1)} %copy-done.5, bf16[256,2,128,1]{0,2,3,1:T(8,128)(2,1)S(1)} %bitcast.67, bf16[256,2,4,128]{3,2,1,0:T(4,128)(2,1)S(1)} %reshape.69), kind=kOutput, calls=%fused_computation.52 | convolution fusion | flops 136315136 | bytes 2826240 | tf_op jit(solution)/shard_map/sub | solution.py:61
  70.1 1.9 %convolution_convert_fusion = bf16[2,128,4,256]{3,1,2,0:T(8,128)(2,1)S(1)} fusion(bf16[256,2,128,1]{0,2,3,1:T(8,128)(2,1)S(1)} %bitcast.68, f32[2,4,256,256]{2,3,1,0:T(8,128)} %get-tuple-element.12, f32[2,4,256]{2,1,0:T(4,128)S(1)} %get-tuple-element.11), kind=kOutput, calls=%fused_computation.10 | convolution fusion | flops 135528448 | bytes 2760704 | tf_op jit(solution)/shard_map/hgij,jhd->ihgd/dot_general | solution.py:65
  72.3 1.9 %collective-permute-start.3 = (bf16[1,256,1024]{2,1,0:T(8,128)(2,1)S(1)}, bf16[1,256,1024]{2,1,0:T(8,128)(2,1)S(1)}, u32[]{:S(2)}, u32[]{:S(2)}) collective-permute-start(bf16[1,256,1024]{2,1,0:T(8,128)(2,1)S(1)} %copy.13), channel_id=1, source_target_pairs={{0,4},{4,8},{8,12},{12,16},{16,20},{20,24},{24,28},{1,5},{5,9},{9,... | collective-permute-start | bytes 1572872 | tf_op jit(solution)/shard_map/ppermute | solution.py:15
  74.2 9.5 %collective-permute-done.3 = bf16[1,256,1024]{2,1,0:T(8,128)(2,1)S(1)} collective-permute-done((bf16[1,256,1024]{2,1,0:T(8,128)(2,1)S(1)}, bf16[1,256,1024]{2,1,0:T(8,128)(2,1)S(1)}, u32[]{:S(2)}, u32[]{:S(2)}) %collective-permute-start.3) | collective-permute-done | bytes 524320 | tf_op jit(solution)/shard_map/ppermute | solution.py:15
  83.7 0.8 copy.44
  (44 shorter events, 5.7 us)
Async XLA Ops:
  0.0 63.2 %copy-start = (bf16[4096,256]{1,0:T(8,128)(2,1)S(1)}, bf16[4096,256]{1,0:T(8,128)(2,1)}, u32[]{:S(2)}) copy-start(bf16[4096,256]{1,0:T(8,128)(2,1)} %param.12) | copy-start | bytes 6291460
  0.0 54.4 %copy-start.1 = (bf16[1,2,64,4096]{3,2,1,0:T(8,128)(2,1)S(1)}, bf16[1,2,64,4096]{3,2,1,0:T(8,128)(2,1)}, u32[]{:S(2)}) copy-start(bf16[1,2,64,4096]{3,2,1,0:T(8,128)(2,1)} %param.7) | copy-start | bytes 3145732
  2.0 15.7 %collective-permute-start = (bf16[64,4096]{1,0:T(8,128)(2,1)S(1)}, bf16[64,4096]{1,0:T(8,128)(2,1)}, u32[]{:S(2)}, u32[]{:S(2)}) collective-permute-start(bf16[64,4096]{1,0:T(8,128)(2,1)S(1)} %dynamic-slice_bitcast_fusion), channel_id=1, source_target_pairs={{0,1},{1,2},{2,3},{3,0},{4,5},{5,6},{6,7},{7,4},{8,9},{9,10},{10,1... | collective-permute-start | bytes 1572872 | tf_op jit(solution)/shard_map/ppermute | solution.py:83
  17.6 15.0 %collective-permute-start.1 = (bf16[64,4096]{1,0:T(8,128)(2,1)}, bf16[64,4096]{1,0:T(8,128)(2,1)}, u32[]{:S(2)}, u32[]{:S(2)}) collective-permute-start(bf16[64,4096]{1,0:T(8,128)(2,1)} %collective-permute-done), channel_id=1, source_target_pairs={{0,1},{1,2},{2,3},{3,0},{4,5},{5,6},{6,7},{7,4},{8,9},{9,10},{10,1... | collective-permute-start | bytes 1572872 | tf_op jit(solution)/shard_map/ppermute | solution.py:83
  32.6 18.4 %collective-permute-start.2 = (bf16[64,4096]{1,0:T(8,128)(2,1)}, bf16[64,4096]{1,0:T(8,128)(2,1)}, u32[]{:S(2)}, u32[]{:S(2)}) collective-permute-start(bf16[64,4096]{1,0:T(8,128)(2,1)} %collective-permute-done.1), channel_id=1, source_target_pairs={{0,1},{1,2},{2,3},{3,0},{4,5},{5,6},{6,7},{7,4},{8,9},{9,10},{10,1... | collective-permute-start | bytes 1572872 | tf_op jit(solution)/shard_map/ppermute | solution.py:83
  53.1 5.4 %copy-start.8 = (bf16[4096,1024]{1,0:T(8,128)(2,1)S(1)}, bf16[4096,1024]{1,0:T(8,128)(2,1)}, u32[]{:S(2)}) copy-start(bf16[4096,1024]{1,0:T(8,128)(2,1)} %param.11) | copy-start | bytes 25165828
  58.1 2.9 %copy-start.2 = (bf16[512,4096]{1,0:T(8,128)(2,1)}, bf16[512,4096]{1,0:T(8,128)(2,1)S(1)}, u32[]{:S(2)}) copy-start(bf16[512,4096]{1,0:T(8,128)(2,1)S(1)} %constant_dynamic-update-slice_fusion) | copy-start | bytes 12582916
  58.6 2.4 %copy-start.6 = (f32[256]{0:T(256)}, f32[256]{0:T(256)S(1)}, u32[]{:S(2)}) copy-start(f32[256]{0:T(256)S(1)} %add_rsqrt_fusion) | copy-start | bytes 3076
  61.2 0.9 %copy-start.4 = (f32[256,128]{1,0:T(8,128)S(1)}, f32[256,128]{1,0:T(8,128)}, u32[]{:S(2)}) copy-start(f32[256,128]{1,0:T(8,128)} %copy.8) | copy-start | bytes 393220
  61.9 1.2 %copy-start.7 = (f32[256]{0:T(256)S(1)}, f32[256]{0:T(256)}, u32[]{:S(2)}) copy-start(f32[256]{0:T(256)} %copy-done.6) | copy-start | bytes 3076
  63.2 3.0 %copy-start.3 = (bf16[512,4096]{1,0:T(8,128)(2,1)S(1)}, bf16[512,4096]{1,0:T(8,128)(2,1)}, u32[]{:S(2)}) copy-start(bf16[512,4096]{1,0:T(8,128)(2,1)} %copy-done.2) | copy-start | bytes 12582916
  63.2 3.5 %copy-start.9 = (bf16[4096,256]{1,0:T(8,128)(2,1)S(1)}, bf16[4096,256]{1,0:T(8,128)(2,1)}, u32[]{:S(2)}) copy-start(bf16[4096,256]{1,0:T(8,128)(2,1)} %param.13) | copy-start | bytes 6291460
  66.1 1.8 %copy-start.5 = (pred[256,256]{0,1:T(8,128)(4,1)S(1)}, pred[256,256]{0,1:T(8,128)(4,1)}, u32[]{:S(2)}) copy-start(pred[256,256]{0,1:T(8,128)(4,1)} %fusion.12) | copy-start | bytes 196612
  72.3 11.4 %collective-permute-start.3 = (bf16[1,256,1024]{2,1,0:T(8,128)(2,1)S(1)}, bf16[1,256,1024]{2,1,0:T(8,128)(2,1)S(1)}, u32[]{:S(2)}, u32[]{:S(2)}) collective-permute-start(bf16[1,256,1024]{2,1,0:T(8,128)(2,1)S(1)} %copy.13), channel_id=1, source_target_pairs={{0,4},{4,8},{8,12},{12,16},{16,20},{20,24},{24,28},{1,5},{5,9},{9,... | collective-permute-start | bytes 1572872 | tf_op jit(solution)/shard_map/ppermute | solution.py:15
